TPU v7x, 32 devices: a whole 2x2x4 slice. The times are simulated.
32 devices in a mesh: section: 4 (over z), mp: 8 (over y, x, core).
Axes of the slice: x: 2, y: 2, z: 4, core: 2. Of those that a mesh axis runs over, the one named last changes fastest.
Arguments:
- embeddings: bfloat16 [4, 4, 128, 4096], P('section', None, None, 'mp'), may hold values from -6 to 6
- stored: bfloat16 [4, 3, 128, 4096], P('section', None, None, 'mp'), may hold values from -6 to 6
- dwa_weights: float32 [4, 4], replicated, may hold values from -2.4 to 2.4
- norm_gain: float32 [4, 4096], P('section'), may hold values from 0.5 to 1.5
- qkv_weight: bfloat16 [4, 4096, 3, 4096], P('section', None, None, 'mp')
- out_weight: bfloat16 [4, 4096, 4096], P('section', None, 'mp'), may hold values from -0.09375 to 0.09375
Outputs:
- layer_outputs: bfloat16 [4, 4, 128, 4096], P('section', None, None, 'mp')
All inputs are finite; a program needn't handle non-finite values.
Results may differ from a plain program's by a relative error of at most 0.014.
Values may be sent and summed in bfloat16 or wider, within the bound.
A program may use at most 64 MiB of HBM per device.

v0:
```python
import jax
import jax.numpy as jnp
from jax import lax
from jax.sharding import PartitionSpec as P

D = 4096
HEAD_DIM = 128


EPS = 1e-06


def attend_heads(projected):
    length = projected.shape[0]
    query = projected[:, 0].astype(jnp.float32)
    key_rows = projected[:, 1].astype(jnp.float32)
    value_rows = projected[:, 2].astype(jnp.float32)
    scores = jnp.einsum("qhd,khd->hqk", query, key_rows) * projected.shape[3] ** (-0.5)
    causal = lax.broadcasted_iota(jnp.int32, (length, length), 0) >= lax.broadcasted_iota(
        jnp.int32, (length, length), 1
    )
    scores = jnp.where(causal[None], scores, -1e30)
    row_max = jnp.max(scores, axis=2, keepdims=True)
    weights = jnp.exp(scores - row_max)
    probs = (weights / jnp.sum(weights, axis=2, keepdims=True)).astype(jnp.bfloat16)
    mixed = jnp.einsum("hqk,khd->qhd", probs.astype(jnp.float32), value_rows)
    return mixed.astype(jnp.bfloat16).reshape(length, -1)


def local(embeddings, stored, dwa_weights, norm_gain, qkv_weight, out_weight):
    sections = lax.axis_size("section")
    section_rank = lax.axis_index("section")
    tick_count = embeddings.shape[1]
    length = embeddings.shape[2]
    shard_width = embeddings.shape[3]
    heads_here = shard_width // HEAD_DIM
    triangle = jnp.tril(jnp.ones((sections, sections), jnp.float32))
    mixing = dwa_weights * triangle
    own_row = lax.dynamic_index_in_dim(mixing, section_rank, 0, keepdims=False)
    history = jnp.concatenate(
        [stored[0], jnp.zeros((tick_count, length, shard_width), jnp.bfloat16)], axis=0
    )
    gain_row = norm_gain[0]
    weight_in = qkv_weight[0].reshape(D, 3 * shard_width)
    weight_out = out_weight[0]
    results = []
    for step_index in range(tick_count):
        own_embed = own_row[0] * embeddings[0, step_index].astype(jnp.float32)
        outgoing = lax.slice_in_dim(history, step_index, step_index + sections, axis=0)[::-1]
        incoming = lax.all_to_all(outgoing, "section", split_axis=0, concat_axis=0, tiled=True)
        summed = own_embed + jnp.tensordot(own_row[1:], incoming[:-1].astype(jnp.float32), axes=1)
        inputs = summed.astype(jnp.bfloat16)
        gathered = lax.all_gather(inputs, "mp", axis=1, tiled=True)
        values = gathered.astype(jnp.float32)
        inverse = lax.rsqrt(jnp.mean(values * values, axis=1, keepdims=True) + EPS)
        normed = (values * inverse * gain_row).astype(jnp.bfloat16)
        projected = jnp.dot(normed, weight_in, preferred_element_type=jnp.float32).astype(
            jnp.bfloat16
        )
        projected = projected.reshape(length, 3, heads_here, HEAD_DIM)
        mixed = attend_heads(projected)
        attn = jnp.dot(
            lax.all_gather(mixed, "mp", axis=1, tiled=True),
            weight_out,
            preferred_element_type=jnp.float32,
        )
        fresh_rows = (inputs.astype(jnp.float32) + attn).astype(jnp.bfloat16)
        slot_index = step_index + sections - 1 - section_rank
        history = lax.dynamic_update_slice_in_dim(history, fresh_rows[None], slot_index, 0)
        results.append(fresh_rows)
    return jnp.stack(results)[None]


def solution(mesh):
    in_specs = (
        P("section", None, None, "mp"),
        P("section", None, None, "mp"),
        P(),
        P("section", None),
        P("section", None, None, "mp"),
        P("section", None, "mp"),
    )
    out_specs = P("section", None, None, "mp")
    return jax.shard_map(local, mesh=mesh, in_specs=in_specs, out_specs=out_specs, check_vma=False)
```

profile of v0, /device:TPU:25, one launch (start us, length us, event | category | flops | bytes accessed | tf_op | source)
XLA Modules:
  0.0 343.5 jit_solution(4346351158753544363)
XLA Ops:
  6.5 1.0 pad_slice_fusion
  8.4 4.5 %all-to-all-start = ((bf16[4,128,512]{2,1,0:T(8,128)(2,1)}), bf16[4,128,512]{2,1,0:T(8,128)(2,1)S(1)}, u32[]{:S(2)}, u32[]{:S(2)}) async-start(bf16[4,128,512]{2,1,0:T(8,128)(2,1)} %rev.12), calls=%async_computation | async-start | bytes 1048576 | tf_op jit(solution)/shard_map/all_to_all | solution.py:50
  13.0 11.2 %all-to-all-done = bf16[4,128,512]{2,1,0:T(8,128)(2,1)S(1)} async-done(((bf16[4,128,512]{2,1,0:T(8,128)(2,1)}), bf16[4,128,512]{2,1,0:T(8,128)(2,1)S(1)}, u32[]{:S(2)}, u32[]{:S(2)}) %all-to-all-start) | async-done | bytes 524320 | tf_op jit(solution)/shard_map/all_to_all | solution.py:50
  25.6 16.9 %copy.23 = bf16[1,4096,3,512]{1,3,2,0:T(8,128)(2,1)} copy(bf16[1,4096,3,512]{3,1,2,0:T(8,128)(2,1)} %param.10) | data formatting | bytes 25165824 | tf_op args[4]
  42.6 9.4 %all-gather.9.cloned.1.call-done = bf16[128,4096]{1,0:T(8,128)(2,1)} async-done(((bf16[128,512]{1,0:T(8,128)(2,1)}), bf16[128,4096]{1,0:T(8,128)(2,1)}) %all-gather.9.cloned.1.call-update) | async-done | bytes 1048592 | tf_op jit(solution)/shard_map/all_gather | solution.py:53
  52.0 1.5 fusion.12
  53.5 9.2 %convolution_convert_fusion.3 = bf16[128,1536]{1,0:T(8,128)(2,1)S(1)} fusion(bf16[4096,1536]{0,1:T(8,128)(2,1)} %bitcast.153, bf16[128,4096]{1,0:T(8,128)(2,1)} %all-gather.9.cloned.1.call-done, f32[4096]{0:T(1024)S(1)} %bitcast.159, f32[128]{0:T(128)S(1)} %add_rsqrt_fusion.3), kind=kOutput, calls=%fused_computation.23 | convolution fusion | flops 1612906496 | bytes 14041600 | tf_op jit(solution)/shard_map/dot_general | solution.py:57
  63.5 0.9 convolution_convert_fusion.7
  64.5 23.4 %all-gather.11.cloned.1.call-done = bf16[128,4096]{0,1:T(8,128)(2,1)} async-done(((bf16[128,512]{0,1:T(8,128)(2,1)}), bf16[128,4096]{0,1:T(8,128)(2,1)}) %all-gather.11.cloned.1.call-update) | async-done | bytes 1048592 | tf_op jit(solution)/shard_map/all_gather | solution.py:63
  87.9 3.3 constant_dynamic-update-slice_fusion.2
  91.2 16.7 %all_to_all.20 = bf16[4,128,512]{2,1,0:T(8,128)(2,1)S(1)} all-to-all(bf16[4,128,512]{2,1,0:T(8,128)(2,1)S(1)} %rev.13), channel_id=1, replica_groups=mesh['section'=4,'mp'=8] {'section'}, dimensions={0} | all-to-all | bytes 1048576 | tf_op jit(solution)/shard_map/all_to_all | solution.py:50
  109.2 24.4 %all-gather.13.cloned.1.call-done = bf16[128,4096]{1,0:T(8,128)(2,1)} async-done(((bf16[128,512]{1,0:T(8,128)(2,1)}), bf16[128,4096]{1,0:T(8,128)(2,1)}) %all-gather.13.cloned.1.call-update) | async-done | bytes 1048592 | tf_op jit(solution)/shard_map/all_gather | solution.py:53
  133.6 1.5 fusion.15
  135.1 9.2 %convolution_convert_fusion.2 = bf16[128,1536]{1,0:T(8,128)(2,1)S(1)} fusion(bf16[4096,1536]{0,1:T(8,128)(2,1)} %bitcast.154, bf16[128,4096]{1,0:T(8,128)(2,1)} %all-gather.13.cloned.1.call-done, f32[128]{0:T(128)S(1)} %add_rsqrt_fusion.2, f32[4096]{0:T(1024)S(1)} %bitcast.160), kind=kOutput, calls=%fused_computation.22 | convolution fusion | flops 1612906496 | bytes 14041600 | tf_op jit(solution)/shard_map/dot_general | solution.py:57
  145.0 0.9 convolution_convert_fusion.6
  146.0 23.5 %all-gather.15.cloned.1.call-done = bf16[128,4096]{0,1:T(8,128)(2,1)} async-done(((bf16[128,512]{0,1:T(8,128)(2,1)}), bf16[128,4096]{0,1:T(8,128)(2,1)}) %all-gather.15.cloned.1.call-update) | async-done | bytes 1048592 | tf_op jit(solution)/shard_map/all_gather | solution.py:63
  169.4 3.3 constant_dynamic-update-slice_fusion.1
  172.8 16.7 %all_to_all.21 = bf16[4,128,512]{2,1,0:T(8,128)(2,1)S(1)} all-to-all(bf16[4,128,512]{2,1,0:T(8,128)(2,1)S(1)} %rev.14), channel_id=1, replica_groups=mesh['section'=4,'mp'=8] {'section'}, dimensions={0} | all-to-all | bytes 1048576 | tf_op jit(solution)/shard_map/all_to_all | solution.py:50
  190.8 24.4 %all-gather.17.cloned.1.call-done = bf16[128,4096]{1,0:T(8,128)(2,1)} async-done(((bf16[128,512]{1,0:T(8,128)(2,1)}), bf16[128,4096]{1,0:T(8,128)(2,1)}) %all-gather.17.cloned.1.call-update) | async-done | bytes 1048592 | tf_op jit(solution)/shard_map/all_gather | solution.py:53
  215.2 1.5 fusion.18
  216.7 9.2 %convolution_convert_fusion.1 = bf16[128,1536]{1,0:T(8,128)(2,1)S(1)} fusion(bf16[4096,1536]{0,1:T(8,128)(2,1)} %bitcast.155, bf16[128,4096]{1,0:T(8,128)(2,1)} %all-gather.17.cloned.1.call-done, f32[128]{0:T(128)S(1)} %add_rsqrt_fusion.1, f32[4096]{0:T(1024)S(1)} %bitcast.161), kind=kOutput, calls=%fused_computation.21 | convolution fusion | flops 1612906496 | bytes 14041600 | tf_op jit(solution)/shard_map/dot_general | solution.py:57
  226.6 0.9 convolution_convert_fusion.5
  227.6 23.4 %all-gather.19.cloned.1.call-done = bf16[128,4096]{0,1:T(8,128)(2,1)} async-done(((bf16[128,512]{0,1:T(8,128)(2,1)}), bf16[128,4096]{0,1:T(8,128)(2,1)}) %all-gather.19.cloned.1.call-update) | async-done | bytes 1048592 | tf_op jit(solution)/shard_map/all_gather | solution.py:63
  251.0 3.3 constant_dynamic-update-slice_fusion
  254.4 16.7 %all_to_all.22 = bf16[4,128,512]{2,1,0:T(8,128)(2,1)S(1)} all-to-all(bf16[4,128,512]{2,1,0:T(8,128)(2,1)S(1)} %rev.15), channel_id=1, replica_groups=mesh['section'=4,'mp'=8] {'section'}, dimensions={0} | all-to-all | bytes 1048576 | tf_op jit(solution)/shard_map/all_to_all | solution.py:50
  272.4 24.4 %all-gather.21.cloned.1.call-done = bf16[128,4096]{1,0:T(8,128)(2,1)} async-done(((bf16[128,512]{1,0:T(8,128)(2,1)}), bf16[128,4096]{1,0:T(8,128)(2,1)}) %all-gather.21.cloned.1.call-update) | async-done | bytes 1048592 | tf_op jit(solution)/shard_map/all_gather | solution.py:53
  296.7 1.5 fusion.21
  298.3 9.2 %convolution_convert_fusion = bf16[128,1536]{1,0:T(8,128)(2,1)S(1)} fusion(bf16[4096,1536]{0,1:T(8,128)(2,1)} %bitcast.156, bf16[128,4096]{1,0:T(8,128)(2,1)} %all-gather.21.cloned.1.call-done, f32[128]{0:T(128)S(1)} %add_rsqrt_fusion, f32[4096]{0:T(1024)S(1)} %bitcast.162), kind=kOutput, calls=%fused_computation.20 | convolution fusion | flops 1612906496 | bytes 14041600 | tf_op jit(solution)/shard_map/dot_general | solution.py:57
  308.2 0.9 convolution_convert_fusion.4
  309.1 23.5 %all-gather.23.cloned.1.call-done = bf16[128,4096]{0,1:T(8,128)(2,1)} async-done(((bf16[128,512]{0,1:T(8,128)(2,1)}), bf16[128,4096]{0,1:T(8,128)(2,1)}) %all-gather.23.cloned.1.call-update) | async-done | bytes 1048592 | tf_op jit(solution)/shard_map/all_gather | solution.py:63
  332.6 3.3 fusion.69
  335.8 0.9 maximum_bitcast_fusion
  (79 shorter events, 9.4 us)
Async XLA Ops:
  6.5 6.4 %copy-start.7 = (f32[4,4]{1,0:T(4,128)S(1)}, f32[4,4]{1,0:T(4,128)}, u32[]{:S(2)}) copy-start(f32[4,4]{1,0:T(4,128)} %param.8) | copy-start | bytes 196
  7.6 17.2 %copy-start.5 = (bf16[1,4,128,512]{3,2,1,0:T(8,128)(2,1)S(1)}, bf16[1,4,128,512]{3,2,1,0:T(8,128)(2,1)}, u32[]{:S(2)}) copy-start(bf16[1,4,128,512]{3,2,1,0:T(8,128)(2,1)} %param.6) | copy-start | bytes 1572868
  8.4 15.8 %all-to-all-start = ((bf16[4,128,512]{2,1,0:T(8,128)(2,1)}), bf16[4,128,512]{2,1,0:T(8,128)(2,1)S(1)}, u32[]{:S(2)}, u32[]{:S(2)}) async-start(bf16[4,128,512]{2,1,0:T(8,128)(2,1)} %rev.12), calls=%async_computation | async-start | bytes 1048576 | tf_op jit(solution)/shard_map/all_to_all | solution.py:50
  13.0 39.0 %all-gather.9.cloned.1.call-start = ((), (), s32[]{:S(2)}) async-start(), calls=%async_computation.4 | async-start | bytes 1179648 | tf_op jit(solution)/shard_map/all_gather | solution.py:53
  25.5 28.0 %copy-start.6 = (f32[1,4096]{1,0:T(1,128)S(1)}, f32[1,4096]{1,0:T(1,128)}, u32[]{:S(2)}) copy-start(f32[1,4096]{1,0:T(1,128)} %param.9) | copy-start | bytes 49156
  25.5 62.3 %all-gather.11.cloned.1.call-start = ((), (), s32[]{:S(2)}) async-start(), calls=%async_computation.5 | async-start | bytes 1179648 | tf_op jit(solution)/shard_map/all_gather | solution.py:63
  62.7 1.7 copy-start
  62.8 25.0 %copy-start.1 = (bf16[128,512]{1,0:T(8,128)(2,1)S(1)}, bf16[128,512]{1,0:T(8,128)(2,1)}, u32[]{:S(2)}) copy-start(bf16[128,512]{1,0:T(8,128)(2,1)} %fusion.95) | copy-start | bytes 393220
  64.4 69.2 %all-gather.13.cloned.1.call-start = ((), (), s32[]{:S(2)}) async-start(), calls=%async_computation.6 | async-start | bytes 1179648 | tf_op jit(solution)/shard_map/all_gather | solution.py:53
  109.2 60.3 %all-gather.15.cloned.1.call-start = ((), (), s32[]{:S(2)}) async-start(), calls=%async_computation.7 | async-start | bytes 1179648 | tf_op jit(solution)/shard_map/all_gather | solution.py:63
  144.3 25.1 %copy-start.3 = (bf16[128,512]{1,0:T(8,128)(2,1)S(1)}, bf16[128,512]{1,0:T(8,128)(2,1)}, u32[]{:S(2)}) copy-start(bf16[128,512]{1,0:T(8,128)(2,1)} %fusion.94) | copy-start | bytes 393220
  145.9 69.2 %all-gather.17.cloned.1.call-start = ((), (), s32[]{:S(2)}) async-start(), calls=%async_computation.8 | async-start | bytes 1179648 | tf_op jit(solution)/shard_map/all_gather | solution.py:53
  190.7 60.3 %all-gather.19.cloned.1.call-start = ((), (), s32[]{:S(2)}) async-start(), calls=%async_computation.9 | async-start | bytes 1179648 | tf_op jit(solution)/shard_map/all_gather | solution.py:63
  225.9 25.1 %copy-start.2 = (bf16[128,512]{1,0:T(8,128)(2,1)S(1)}, bf16[128,512]{1,0:T(8,128)(2,1)}, u32[]{:S(2)}) copy-start(bf16[128,512]{1,0:T(8,128)(2,1)} %fusion.93) | copy-start | bytes 393220
  227.5 69.2 %all-gather.21.cloned.1.call-start = ((), (), s32[]{:S(2)}) async-start(), calls=%async_computation.10 | async-start | bytes 1179648 | tf_op jit(solution)/shard_map/all_gather | solution.py:53
  272.3 60.3 %all-gather.23.cloned.1.call-start = ((), (), s32[]{:S(2)}) async-start(), calls=%async_computation.11 | async-start | bytes 1179648 | tf_op jit(solution)/shard_map/all_gather | solution.py:63
  307.5 25.1 %copy-start.4 = (bf16[128,512]{1,0:T(8,128)(2,1)S(1)}, bf16[128,512]{1,0:T(8,128)(2,1)}, u32[]{:S(2)}) copy-start(bf16[128,512]{1,0:T(8,128)(2,1)} %fusion.92) | copy-start | bytes 393220
Sparse Core Ops, SparseCore 0:
  25.7 26.2 all-gather.8
  64.5 23.3 all-gather.10
  109.3 24.2 all-gather.12
  146.0 23.3 all-gather.14
  190.9 24.2 all-gather.16
  227.6 23.3 all-gather.18
  272.4 24.2 all-gather.20
  309.2 23.3 all-gather.22
where the time goes:
time: 346 us; the launch traced here: 344 us
  waiting for transfers between devices  188 us (54%)
  matrix products  56.3 us (16%)
  blocking collectives  50 us (14%)
  local copies, waits for them, and re-layouts  20.7 us (6%)
  between operations  13.9 us (4%)
  other arithmetic  10.2 us (3%)
  starting transfers between devices  4.82 us (1%)
    all_gather x4, waiting for transfers between devices, local(): lax.all_gather(mixed, 'mp', axis=1, tiled=True)  93.8 us
    all_gather x4, waiting for transfers between devices, local(): gathered = lax.all_gather(inputs, 'mp', axis=1, tiled=True)  82.5 us
    all_to_all x3, blocking collectives, local(): lax.all_to_all(outgoing, 'section', split_axis=0, concat_axis=0, tiled=True)  50 us
    dot_general x4, matrix products, local(): jnp.dot(normed, weight_in, preferred_element_type=jnp.float32)  36.9 us
    unnamed x21, local copies, waits for them, and re-layouts  17.5 us
    dot_general x4, matrix products, local(): jnp.dot(lax.all_gather(mixed, 'mp', axis=1, tiled=True), weight_out, pref...  13 us
    all_to_all x1, waiting for transfers between devices, local(): lax.all_to_all(outgoing, 'section', split_axis=0, concat_axis=0, tiled=True)  11.2 us
  transfers between devices with their start and end apart: 9, of which 9 were waited for; matrix products, arithmetic and copies ran while one was open for 5% of the time, Pallas kernels for 0%

commit v1 on v0

v1 whole, which is shorter than its diff:
```python
import functools

import jax
import jax.numpy as jnp
from jax import lax
from jax.experimental import pallas as pl
from jax.experimental.pallas import tpu as pltpu
from jax.sharding import PartitionSpec as P

HEAD_DIM = 128
EPS = 1e-06
MESH = pl.DeviceIdType.MESH


def kernel(sections, ranks, groups, mixing, gain, emb_hbm, stored, wqkv_hbm, wout_hbm, out,
           wqkv, wout, emb, rx, xg, hg, summed, acc, acc_out, ssq,
           wqkv_sem, wout_sem, emb_sem, zst_send, zsend, zrecv, xsend, xrecv, hsend, hrecv):
    k = lax.axis_index("section")
    me = lax.axis_index("mp")
    ticks, length, width = emb.shape
    features = width * ranks
    chips = ranks // 2
    chip, core = me // 2, lax.rem(me, 2)
    sib = chip * 2 + 1 - core
    gw = width // groups

    def same(dc):
        return lax.rem(chip + dc, chips) * 2 + core

    def src(dc):
        return lax.rem(chip - dc + chips, chips) * 2 + core

    def sib_src(dc):
        return lax.rem(chip - dc + chips, chips) * 2 + 1 - core

    def rows(blk):
        return pl.ds(pl.multiple_of(blk * width, width), width)

    def load_wqkv(blk):
        return pltpu.make_async_copy(wqkv_hbm.at[:, rows(blk), :], wqkv.at[:, rows(blk), :], wqkv_sem.at[blk])

    emb_copy = pltpu.make_async_copy(emb_hbm, emb, emb_sem)
    wout_copy = pltpu.make_async_copy(wout_hbm, wout, wout_sem)
    emb_copy.start()
    load_wqkv(me).start()
    load_wqkv(sib).start()
    for dc in range(1, chips):
        load_wqkv(src(dc)).start()
    for dc in range(1, chips):
        load_wqkv(sib_src(dc)).start()
    wout_copy.start()

    barrier = pltpu.get_barrier_semaphore()
    for dc in range(1, chips):
        pl.semaphore_signal(barrier, inc=1, device_id=(k, same(dc)), device_id_type=MESH)
    pl.semaphore_signal(barrier, inc=1, device_id=(k, sib), device_id_type=MESH)
    for d in range(1, sections):
        pl.semaphore_signal(barrier, inc=1, device_id=(lax.rem(k + d, sections), me), device_id_type=MESH)
    pl.semaphore_wait(barrier, chips + sections - 1)

    def stored_send(d, t):
        slot = jnp.maximum(t - k - d + sections - 1, 0)
        return pltpu.make_async_remote_copy(
            src_ref=stored.at[slot], dst_ref=rx.at[d - 1, t], send_sem=zst_send.at[d - 1, t],
            recv_sem=zrecv.at[d - 1, t], device_id=(lax.rem(k + d, sections), me), device_id_type=MESH)

    def fresh_send(d, t):
        return pltpu.make_async_remote_copy(
            src_ref=out.at[t], dst_ref=rx.at[d - 1, t + d], send_sem=zsend.at[d - 1, t],
            recv_sem=zrecv.at[d - 1, t + d], device_id=(lax.rem(k + d, sections), me), device_id_type=MESH)

    def fresh_recv(d, t):
        return pltpu.make_async_remote_copy(
            src_ref=out.at[t], dst_ref=rx.at[d - 1, t], send_sem=zsend.at[d - 1, t],
            recv_sem=zrecv.at[d - 1, t], device_id=(lax.rem(k + d, sections), me), device_id_type=MESH)

    for t in range(ticks):
        for d in range(t + 1, sections):
            @pl.when(k + d < sections)
            def _():
                stored_send(d, t).start()

    emb_copy.wait()

    causal = lax.broadcasted_iota(jnp.int32, (length, length), 0) >= lax.broadcasted_iota(
        jnp.int32, (length, length), 1)

    def x_copy(t, blk, send_at, recv_at, target):
        return pltpu.make_async_remote_copy(
            src_ref=xg.at[t, blk], dst_ref=xg.at[t, blk], send_sem=xsend.at[send_at],
            recv_sem=xrecv.at[recv_at], device_id=(k, target), device_id_type=MESH)

    def h_copy(t, g, blk, send_at, recv_at, target):
        return pltpu.make_async_remote_copy(
            src_ref=hg.at[t, g, blk], dst_ref=hg.at[t, g, blk], send_sem=hsend.at[g, send_at],
            recv_sem=hrecv.at[g, recv_at], device_id=(k, target), device_id_type=MESH)

    def tick(t, carry):
        summed[...] = mixing[k, 0] * emb[t].astype(jnp.float32)
        for d in range(sections - 1, 0, -1):
            @pl.when(d <= k)
            def _():
                fresh_recv(d, t).wait_recv()
                summed[...] += mixing[k, jnp.maximum(k - d + 1, 0)] * rx[d - 1, t].astype(jnp.float32)
        xg[t, me] = summed[...].astype(jnp.bfloat16)
        for dc in range(1, chips):
            x_copy(t, me, dc, dc, same(dc)).start()
        x_copy(t, me, chips, chips, sib).start()

        def consume(blk, first=False):
            @pl.when(t == 0)
            def _():
                load_wqkv(blk).wait()
            values = xg[t, blk].astype(jnp.float32)
            part = jnp.sum(values * values, axis=1, keepdims=True)
            scaled = (values * gain[:, rows(blk)]).astype(jnp.bfloat16)
            if first:
                ssq[...] = part
            else:
                ssq[...] += part
            for j in range(3):
                prod = jnp.dot(scaled, wqkv[j, rows(blk), :], preferred_element_type=jnp.float32)
                if first:
                    acc[j] = prod
                else:
                    acc[j] += prod

        consume(me, True)
        x_copy(t, sib, chips, chips, sib).wait_recv()
        consume(sib)

        def direct(dc, c):
            blk = src(dc)
            x_copy(t, blk, dc, dc, sib).wait_recv()
            x_copy(t, blk, chips + dc, chips + dc, sib).start()
            consume(blk)
            return c

        def relayed(dc, c):
            blk = sib_src(dc)
            x_copy(t, blk, chips + dc, chips + dc, sib).wait_recv()
            consume(blk)
            return c

        lax.fori_loop(1, chips, direct, 0)
        lax.fori_loop(1, chips, relayed, 0)

        inverse = lax.rsqrt(ssq[...] * (1.0 / features) + EPS)
        for g in range(groups):
            for h in range(gw // HEAD_DIM):
                cols = pl.ds(g * gw + h * HEAD_DIM, HEAD_DIM)
                q = (acc[0, :, cols] * inverse).astype(jnp.bfloat16)
                kk = (acc[1, :, cols] * inverse).astype(jnp.bfloat16)
                v = (acc[2, :, cols] * inverse).astype(jnp.bfloat16)
                scores = lax.dot_general(q, kk, (((1,), (1,)), ((), ())), preferred_element_type=jnp.float32)
                scores = jnp.where(causal, scores * HEAD_DIM ** -0.5, -1e30)
                weights = jnp.exp(scores - jnp.max(scores, axis=1, keepdims=True))
                probs = (weights / jnp.sum(weights, axis=1, keepdims=True)).astype(jnp.bfloat16)
                mixed = jnp.dot(probs, v, preferred_element_type=jnp.float32).astype(jnp.bfloat16)
                hg[t, g, me, :, pl.ds(h * HEAD_DIM, HEAD_DIM)] = mixed
            for dc in range(1, chips):
                h_copy(t, g, me, dc, dc, same(dc)).start()
            h_copy(t, g, me, chips, chips, sib).start()

        @pl.when(t == 0)
        def _():
            wout_copy.wait()

        def consume_h(g, blk):
            part = pl.ds(pl.multiple_of(blk * width + g * gw, gw), gw)
            acc_out[...] += jnp.dot(hg[t, g, blk], wout[part, :], preferred_element_type=jnp.float32)

        acc_out[...] = xg[t, me].astype(jnp.float32)
        for g in range(groups):
            consume_h(g, me)
        for g in range(groups):
            h_copy(t, g, sib, chips, chips, sib).wait_recv()
            consume_h(g, sib)
        for g in range(groups):
            def h_direct(dc, c):
                blk = src(dc)
                h_copy(t, g, blk, dc, dc, sib).wait_recv()
                h_copy(t, g, blk, chips + dc, chips + dc, sib).start()
                consume_h(g, blk)
                return c

            def h_relayed(dc, c):
                blk = sib_src(dc)
                h_copy(t, g, blk, chips + dc, chips + dc, sib).wait_recv()
                consume_h(g, blk)
                return c

            lax.fori_loop(1, chips, h_direct, 0)
            lax.fori_loop(1, chips, h_relayed, 0)

        out[t] = acc_out[...].astype(jnp.bfloat16)
        for d in range(1, min(sections, ticks)):
            @pl.when((t + d < ticks) & (k + d < sections))
            def _():
                fresh_send(d, t).start()

        def drain(i, c):
            x_copy(t, me, i, i, sib).wait_send()
            for g in range(groups):
                h_copy(t, g, me, i, i, sib).wait_send()
            return c

        lax.fori_loop(1, ranks, drain, 0)
        return carry

    lax.fori_loop(0, ticks, tick, 0)

    for t in range(ticks):
        for d in range(1, sections):
            @pl.when(k + d < sections)
            def _():
                if t < d:
                    stored_send(d, t).wait_send()
                if t + d < ticks:
                    fresh_send(d, t).wait_send()


def local(sections, ranks, embeddings, stored, dwa_weights, norm_gain, qkv_weight, out_weight):
    _, ticks, length, width = embeddings.shape
    features = width * ranks
    heads_here = width // HEAD_DIM
    groups = 2 if heads_here % 2 == 0 else 1
    bf16, f32 = jnp.bfloat16, jnp.float32
    wqkv = jnp.transpose(qkv_weight[0], (1, 0, 2))
    dma = pltpu.SemaphoreType.DMA
    anywhere = pl.BlockSpec(memory_space=pl.ANY)
    result = pl.pallas_call(
        functools.partial(kernel, sections, ranks, groups),
        out_shape=jax.ShapeDtypeStruct((ticks, length, width), bf16),
        in_specs=[pl.BlockSpec(memory_space=pltpu.SMEM), pl.BlockSpec(memory_space=pltpu.VMEM)] + [anywhere] * 4,
        out_specs=pl.BlockSpec(memory_space=pltpu.VMEM),
        scratch_shapes=[
            pltpu.VMEM((3, features, width), bf16),
            pltpu.VMEM((features, width), bf16),
            pltpu.VMEM((ticks, length, width), bf16),
            pltpu.VMEM((sections - 1, ticks, length, width), bf16),
            pltpu.VMEM((ticks, ranks, length, width), bf16),
            pltpu.VMEM((ticks, groups, ranks, length, width // groups), bf16),
            pltpu.VMEM((length, width), f32),
            pltpu.VMEM((3, length, width), f32),
            pltpu.VMEM((length, width), f32),
            pltpu.VMEM((length, 1), f32),
            dma((ranks,)), dma, dma,
            dma((sections - 1, ticks)), dma((sections - 1, ticks)), dma((sections - 1, ticks)),
            dma((ranks,)), dma((ranks,)), dma((groups, ranks)), dma((groups, ranks)),
        ],
        compiler_params=pltpu.CompilerParams(
            collective_id=0, has_side_effects=True, vmem_limit_bytes=60 * 1024 * 1024),
    )(dwa_weights, norm_gain, embeddings[0], stored[0], wqkv, out_weight[0])
    return result[None]


def solution(mesh):
    in_specs = (
        P("section", None, None, "mp"),
        P("section", None, None, "mp"),
        P(),
        P("section", None),
        P("section", None, None, "mp"),
        P("section", None, "mp"),
    )
    out_specs = P("section", None, None, "mp")
    body = functools.partial(local, mesh.shape["section"], mesh.shape["mp"])
    return jax.shard_map(body, mesh=mesh, in_specs=in_specs, out_specs=out_specs, check_vma=False)
```

time: 346 us -> 108 us (0.31)
  waiting for transfers between devices: 188 us -> 0 us
  Pallas kernels: 0 us -> 106 us
  matrix products: 56.3 us -> 0 us
  blocking collectives: 50 us -> 0 us
  local copies, waits for them, and re-layouts: 20.7 us -> 1.87 us
  between operations: 13.9 us -> 0.01 us
  other arithmetic: 10.2 us -> 0 us
  starting transfers between devices: 4.82 us -> 0 us
    all_gather x8 -> x0, waiting for transfers between devices: 176 us -> none  [the longest x4 93.8 us: local(): lax.all_gather(mixed, 'mp', axis=1, tiled=True)]
    pallas_call x0 -> x1, Pallas kernels: none -> 106 us  [local(): pl.pallas_call(functools.partial(kernel, sections, ranks, groups), out_sh...]
    dot_general x20 -> x0, matrix products: 56.3 us -> none  [the longest x4 36.9 us: local(): jnp.dot(normed, weight_in, preferred_element_type=jnp.float32)]
    all_to_all x3 -> x0, blocking collectives: 50 us -> none  [local(): lax.all_to_all(outgoing, 'section', split_axis=0, concat_axis=0, tiled=True)]
    unnamed x21 -> x1, local copies, waits for them, and re-layouts: 17.5 us -> 1.87 us
    all_to_all x1 -> x0, waiting for transfers between devices: 11.2 us -> none  [local(): lax.all_to_all(outgoing, 'section', split_axis=0, concat_axis=0, tiled=True)]
    reduce_sum x4 -> x0, other arithmetic: 6.07 us -> none  [local(): inverse = lax.rsqrt(jnp.mean(values * values, axis=1, keepdims=True) + EPS)]
    all_to_all x1 -> x0, starting transfers between devices: 4.53 us -> none  [local(): lax.all_to_all(outgoing, 'section', split_axis=0, concat_axis=0, tiled=True)]
  transfers between devices with their start and end apart: 9 -> 0, of which waited for: 9 -> 0; matrix products, arithmetic and copies ran while one was open for 5% -> 0% of each run, Pallas kernels for 0% -> 0%
where the time goes in v1:
time: 108 us
  Pallas kernels  106 us (98%)
  local copies, waits for them, and re-layouts  1.87 us (2%)
    pallas_call x1, Pallas kernels, local(): pl.pallas_call(functools.partial(kernel, sections, ranks, groups), out_sh...  106 us

profile of v1, /device:TPU:25, one launch (start us, length us, event | category | flops | bytes accessed | tf_op | source)
XLA Modules:
  0.0 107.7 jit_solution(17696723722802832503)
XLA Ops:
  0.0 105.8 %shard_map.64 = bf16[4,128,512]{2,1,0:T(8,128)(2,1)} custom-call(f32[4,4]{1,0:T(4,128)} %mixing.1, f32[1,4096]{1,0:T(1,128)} %gain.1, bf16[4,128,512]{2,1,0:T(8,128)(2,1)} %bitcast.10, bf16[3,128,512]{2,1,0:T(8,128)(2,1)} %bitcast.11, bf16[3,4096,512]{2,1,0:T(8,128)(2,1)} %bitcast.7, bf16[4096,512]{1,0:T(8,128)(2,1)} %bitcast.8), custom_call_target="tpu_custom_call" | custom-call | tf_op jit(solution)/shard_map/pallas_call | solution.py:232
  105.8 1.9 %copy.8 = bf16[1,4,128,512]{3,2,1,0:T(8,128)(2,1)} copy(bf16[1,4,128,512]{3,2,1,0:T(8,128)(2,1)} %bitcast.9) | data formatting | bytes 1048576

commit v2 on v1

v2 whole, which is shorter than its diff:
```python
import functools

import jax
import jax.numpy as jnp
from jax import lax
from jax.experimental import pallas as pl
from jax.experimental.pallas import tpu as pltpu
from jax.sharding import PartitionSpec as P

HEAD_DIM = 128
EPS = 1e-06
PARTS = 2
MESH = pl.DeviceIdType.MESH


def kernel(sections, ranks, parts, mixing, gain, emb_hbm, stored, wqkv_hbm, wout_hbm, out,
           wqkv, wout, emb, rx, xg, hg, summed, acc, proj, acc_out, ssq,
           wqkv_sem, wout_sem, emb_sem, zst_send, zsend, zrecv, xsend, xrecv, hsend, hrecv):
    k = lax.axis_index("section")
    me = lax.axis_index("mp")
    ticks, length, width = emb.shape
    features = width * ranks
    chips = ranks // 2
    chip, core = me // 2, lax.rem(me, 2)
    sib = chip * 2 + 1 - core
    hr = length // parts

    def same(dc):
        return lax.rem(chip + dc, chips) * 2 + core

    def src(dc):
        return lax.rem(chip - dc + chips, chips) * 2 + core

    def sib_src(dc):
        return lax.rem(chip - dc + chips, chips) * 2 + 1 - core

    def rows(blk):
        return pl.ds(pl.multiple_of(blk * width, width), width)

    def load_wqkv(blk):
        return pltpu.make_async_copy(wqkv_hbm.at[:, rows(blk), :], wqkv.at[:, rows(blk), :], wqkv_sem.at[blk])

    emb_copy = pltpu.make_async_copy(emb_hbm, emb, emb_sem)
    wout_copy = pltpu.make_async_copy(wout_hbm, wout, wout_sem)
    emb_copy.start()
    load_wqkv(me).start()
    load_wqkv(sib).start()
    for dc in range(1, chips):
        load_wqkv(src(dc)).start()
    for dc in range(1, chips):
        load_wqkv(sib_src(dc)).start()
    wout_copy.start()

    barrier = pltpu.get_barrier_semaphore()
    for dc in range(1, chips):
        pl.semaphore_signal(barrier, inc=1, device_id=(k, same(dc)), device_id_type=MESH)
    pl.semaphore_signal(barrier, inc=1, device_id=(k, sib), device_id_type=MESH)
    for d in range(1, sections):
        pl.semaphore_signal(barrier, inc=1, device_id=(lax.rem(k + d, sections), me), device_id_type=MESH)
    pl.semaphore_wait(barrier, chips + sections - 1)

    def span(p):
        return pl.ds(p * hr, hr)

    def section_copy(source, at, d, t, p, sems, send_t):
        return pltpu.make_async_remote_copy(
            src_ref=source.at[at, span(p)], dst_ref=rx.at[d - 1, t, span(p)], send_sem=sems.at[d - 1, send_t, p],
            recv_sem=zrecv.at[d - 1, t, p], device_id=(lax.rem(k + d, sections), me), device_id_type=MESH)

    def stored_send(d, t, p):
        return section_copy(stored, jnp.maximum(t - k - d + sections - 1, 0), d, t, p, zst_send, t)

    def fresh_send(d, t, p):
        return section_copy(out, t, d, t + d, p, zsend, t)

    def section_recv(d, t, p):
        return section_copy(out, t, d, t, p, zsend, t)

    def send_stored(low, high):
        for t in range(low, high):
            for p in range(parts):
                for d in range(t + 1, sections):
                    @pl.when(k + d < sections)
                    def _():
                        stored_send(d, t, p).start()

    send_stored(0, 1)

    emb_copy.wait()

    def x_copy(t, p, blk, send_at, recv_at, target):
        return pltpu.make_async_remote_copy(
            src_ref=xg.at[t, blk, span(p)], dst_ref=xg.at[t, blk, span(p)], send_sem=xsend.at[p, send_at],
            recv_sem=xrecv.at[p, recv_at], device_id=(k, target), device_id_type=MESH)

    def h_copy(t, p, blk, send_at, recv_at, target):
        return pltpu.make_async_remote_copy(
            src_ref=hg.at[t, blk, span(p)], dst_ref=hg.at[t, blk, span(p)], send_sem=hsend.at[p, send_at],
            recv_sem=hrecv.at[p, recv_at], device_id=(k, target), device_id_type=MESH)

    def spread(copy, t, p):
        for dc in range(1, chips):
            copy(t, p, me, dc, dc, same(dc)).start()
        copy(t, p, me, chips, chips, sib).start()

    def gather(copy, consume, t, p, early):
        def forward(dc):
            copy(t, p, src(dc), dc, dc, sib).wait_recv()
            copy(t, p, src(dc), chips + dc, chips + dc, sib).start()

        if early:
            for dc in range(1, chips):
                forward(dc)
        consume(me, True)
        copy(t, p, sib, chips, chips, sib).wait_recv()
        consume(sib)

        def direct(dc, c):
            if not early:
                forward(dc)
            consume(src(dc))
            return c

        def relayed(dc, c):
            copy(t, p, sib_src(dc), chips + dc, chips + dc, sib).wait_recv()
            consume(sib_src(dc))
            return c

        lax.fori_loop(1, chips, direct, 0, unroll=chips <= 4)
        lax.fori_loop(1, chips, relayed, 0, unroll=chips <= 4)

    def tick(t, carry):
        for p in range(parts):
            at = span(p)
            summed[at] = mixing[k, 0] * emb[t, at].astype(jnp.float32)
            for d in range(sections - 1, 0, -1):
                @pl.when(d <= k)
                def _():
                    section_recv(d, t, p).wait_recv()
                    summed[at] += mixing[k, jnp.maximum(k - d + 1, 0)] * rx[d - 1, t, at].astype(jnp.float32)
            xg[t, me, at] = summed[at].astype(jnp.bfloat16)
            spread(x_copy, t, p)

        @pl.when(t == 0)
        def _():
            send_stored(1, ticks)

        for p in range(parts):
            at = span(p)

            def consume(blk, first=False):
                if p == 0:
                    @pl.when(t == 0)
                    def _():
                        load_wqkv(blk).wait()
                values = xg[t, blk, at].astype(jnp.float32)
                part = jnp.sum(values * values, axis=1, keepdims=True)
                scaled = (values * gain[:, rows(blk)]).astype(jnp.bfloat16)
                if first:
                    ssq[at] = part
                else:
                    ssq[at] += part
                for j in range(3):
                    prod = jnp.dot(scaled, wqkv[j, rows(blk), :], preferred_element_type=jnp.float32)
                    if first:
                        acc[j, at] = prod
                    else:
                        acc[j, at] += prod

            gather(x_copy, consume, t, p, p > 0)

            inverse = lax.rsqrt(ssq[at] * (1.0 / features) + EPS)
            seen = (p + 1) * hr
            causal = p * hr + lax.broadcasted_iota(jnp.int32, (hr, seen), 0) >= lax.broadcasted_iota(
                jnp.int32, (hr, seen), 1)
            for j in range(3):
                proj[j, at] = (acc[j, at] * inverse).astype(jnp.bfloat16)
            for h in range(width // HEAD_DIM):
                cols = pl.ds(h * HEAD_DIM, HEAD_DIM)
                scores = lax.dot_general(proj[0, at, cols], proj[1, pl.ds(0, seen), cols], (((1,), (1,)), ((), ())),
                                         preferred_element_type=jnp.float32)
                scores = jnp.where(causal, scores * HEAD_DIM ** -0.5, -1e30)
                weights = jnp.exp(scores - jnp.max(scores, axis=1, keepdims=True))
                probs = (weights / jnp.sum(weights, axis=1, keepdims=True)).astype(jnp.bfloat16)
                mixed = jnp.dot(probs, proj[2, pl.ds(0, seen), cols], preferred_element_type=jnp.float32)
                hg[t, me, at, cols] = mixed.astype(jnp.bfloat16)
            spread(h_copy, t, p)

        @pl.when(t == 0)
        def _():
            wout_copy.wait()

        for p in range(parts):
            at = span(p)

            def consume_h(blk, first=False):
                prod = jnp.dot(hg[t, blk, at], wout[rows(blk), :], preferred_element_type=jnp.float32)
                if first:
                    acc_out[at] = xg[t, me, at].astype(jnp.float32) + prod
                else:
                    acc_out[at] += prod

            gather(h_copy, consume_h, t, p, p > 0)
            out[t, at] = acc_out[at].astype(jnp.bfloat16)
            for d in range(1, min(sections, ticks)):
                @pl.when((t + d < ticks) & (k + d < sections))
                def _():
                    fresh_send(d, t, p).start()

        def drain(i, c):
            for p in range(parts):
                x_copy(t, p, me, i, i, sib).wait_send()
                h_copy(t, p, me, i, i, sib).wait_send()
            return c

        lax.fori_loop(1, ranks, drain, 0)
        return carry

    lax.fori_loop(0, ticks, tick, 0)

    for t in range(ticks):
        for d in range(1, sections):
            @pl.when(k + d < sections)
            def _():
                for p in range(parts):
                    if t < d:
                        stored_send(d, t, p).wait_send()
                    if t + d < ticks:
                        fresh_send(d, t, p).wait_send()


def local(sections, ranks, embeddings, stored, dwa_weights, norm_gain, qkv_weight, out_weight):
    _, ticks, length, width = embeddings.shape
    features = width * ranks
    parts = PARTS
    bf16, f32 = jnp.bfloat16, jnp.float32
    wqkv = jnp.transpose(qkv_weight[0], (1, 0, 2))
    dma = pltpu.SemaphoreType.DMA
    anywhere = pl.BlockSpec(memory_space=pl.ANY)
    result = pl.pallas_call(
        functools.partial(kernel, sections, ranks, parts),
        out_shape=jax.ShapeDtypeStruct((ticks, length, width), bf16),
        in_specs=[pl.BlockSpec(memory_space=pltpu.SMEM), pl.BlockSpec(memory_space=pltpu.VMEM)] + [anywhere] * 4,
        out_specs=pl.BlockSpec(memory_space=pltpu.VMEM),
        scratch_shapes=[
            pltpu.VMEM((3, features, width), bf16),
            pltpu.VMEM((features, width), bf16),
            pltpu.VMEM((ticks, length, width), bf16),
            pltpu.VMEM((sections - 1, ticks, length, width), bf16),
            pltpu.VMEM((ticks, ranks, length, width), bf16),
            pltpu.VMEM((ticks, ranks, length, width), bf16),
            pltpu.VMEM((length, width), f32),
            pltpu.VMEM((3, length, width), f32),
            pltpu.VMEM((3, length, width), bf16),
            pltpu.VMEM((length, width), f32),
            pltpu.VMEM((length, 1), f32),
            dma((ranks,)), dma, dma,
            dma((sections - 1, ticks, parts)), dma((sections - 1, ticks, parts)), dma((sections - 1, ticks, parts)),
            dma((parts, ranks)), dma((parts, ranks)), dma((parts, ranks)), dma((parts, ranks)),
        ],
        compiler_params=pltpu.CompilerParams(
            collective_id=0, has_side_effects=True, vmem_limit_bytes=60 * 1024 * 1024),
    )(dwa_weights, norm_gain, embeddings[0], stored[0], wqkv, out_weight[0])
    return result[None]


def solution(mesh):
    in_specs = (
        P("section", None, None, "mp"),
        P("section", None, None, "mp"),
        P(),
        P("section", None),
        P("section", None, None, "mp"),
        P("section", None, "mp"),
    )
    out_specs = P("section", None, None, "mp")
    body = functools.partial(local, mesh.shape["section"], mesh.shape["mp"])
    return jax.shard_map(body, mesh=mesh, in_specs=in_specs, out_specs=out_specs, check_vma=False)
```

time: 108 us -> 104 us (0.963)
  Pallas kernels: 106 us -> 101 us
    pallas_call x1, Pallas kernels: 106 us -> 101 us  [local(): pl.pallas_call(functools.partial(kernel, sections, ranks, parts), out_sha...]
where the time goes in v2:
time: 104 us; the launch traced here: 103 us
  Pallas kernels  101 us (97%)
  local copies, waits for them, and re-layouts  1.87 us (2%)
    pallas_call x1, Pallas kernels, local(): pl.pallas_call(functools.partial(kernel, sections, ranks, parts), out_sha...  101 us

profile of v2, /device:TPU:25, one launch (start us, length us, event | category | flops | bytes accessed | tf_op | source)
XLA Modules:
  0.0 103.3 jit_solution(1276328291312579021)
XLA Ops:
  0.0 101.5 %shard_map.64 = bf16[4,128,512]{2,1,0:T(8,128)(2,1)} custom-call(f32[4,4]{1,0:T(4,128)} %mixing.1, f32[1,4096]{1,0:T(1,128)} %gain.1, bf16[4,128,512]{2,1,0:T(8,128)(2,1)} %bitcast.10, bf16[3,128,512]{2,1,0:T(8,128)(2,1)} %bitcast.11, bf16[3,4096,512]{2,1,0:T(8,128)(2,1)} %bitcast.7, bf16[4096,512]{1,0:T(8,128)(2,1)} %bitcast.8), custom_call_target="tpu_custom_call" | custom-call | tf_op jit(solution)/shard_map/pallas_call | solution.py:240
  101.5 1.9 %copy.8 = bf16[1,4,128,512]{3,2,1,0:T(8,128)(2,1)} copy(bf16[1,4,128,512]{3,2,1,0:T(8,128)(2,1)} %bitcast.9) | data formatting | bytes 1048576
